TPU v7x, 32 devices: a whole 2x2x4 slice. The times are simulated.
32 devices in a mesh: dp: 32 (over z, y, x, core).
Axes of the slice: x: 2, y: 2, z: 4, core: 2. Of those that a mesh axis runs over, the one named last changes fastest.
Arguments:
- u_norm: bfloat16 [16, 2048, 4096], P(None, 'dp')
- expert_idx: int32 [16, 2048, 2], P(None, 'dp')
- expert_out: bfloat16 [16, 2048, 2, 4096], P(None, 'dp')
- d_out: bfloat16 [16, 2048, 4096], P(None, 'dp')
- w_router: bfloat16 [16, 4096, 16], replicated
Outputs:
- output 1: float32 [], replicated
- output 2: float32 [16, 4096, 16], replicated
- output 3: bfloat16 [16, 2048, 4096], P(None, 'dp')
All inputs are finite; a program needn't handle non-finite values.
Results may differ from a plain program's by a relative error of at most 0.00944661.
Values sent between devices are 32-bit elements.
A program may use at most 1 GiB of HBM per device.

v0:
```python
import jax
import jax.numpy as jnp
from jax import lax
from jax.sharding import PartitionSpec as P

AUX_COEF = 0.02


def router_forward(u_norm, expert_idx, expert_out, d_out, w_router):
    num_exp = w_router.shape[2]
    one_hot = (expert_idx[..., None] == jnp.arange(num_exp)).astype(jnp.float32)
    logits = jnp.einsum('ltd,lde->lte', u_norm, w_router, preferred_element_type=jnp.float32)
    prob_vals = jax.nn.softmax(logits, axis=-1)
    chosen = jnp.sum(one_hot * logits[:, :, None, :], axis=-1)
    gate_vals = jax.nn.softmax(chosen, axis=-1)
    slot_dots = jnp.einsum('ltkd,ltd->ltk', expert_out, d_out, preferred_element_type=jnp.float32)
    return one_hot, prob_vals, gate_vals, slot_dots


def logit_grad(one_hot, prob_vals, gate_vals, slot_dots, aux_pull, loss_scale):
    d_dots = loss_scale * slot_dots
    d_chosen = gate_vals * (d_dots - jnp.sum(gate_vals * d_dots, axis=-1, keepdims=True))
    pull_row = aux_pull[:, None, :]
    aux_grad = prob_vals * (pull_row - jnp.sum(prob_vals * pull_row, axis=-1, keepdims=True))
    return jnp.sum(d_chosen[..., None] * one_hot, axis=2) + aux_grad


def solution(mesh):
    group_size = mesh.shape['dp']

    def local_step(u_norm, expert_idx, expert_out, d_out, w_router):
        num_exp = w_router.shape[2]
        top_k = expert_idx.shape[2]
        tok_all = u_norm.shape[1] * group_size
        one_hot, prob_vals, gate_vals, slot_dots = router_forward(u_norm, expert_idx, expert_out, d_out, w_router)
        local_stats = jnp.concatenate([jnp.sum(one_hot, axis=(1, 2)), jnp.sum(prob_vals, axis=1)], axis=-1)
        glob_stats = lax.psum(local_stats, 'dp')
        exp_frac = glob_stats[:, :num_exp] / (top_k * tok_all)
        prob_mean = glob_stats[:, num_exp:] / tok_all
        aux_total = AUX_COEF * num_exp * jnp.sum(exp_frac * prob_mean)
        main_part = jnp.sum(gate_vals * slot_dots)
        d_logits = logit_grad(one_hot, prob_vals, gate_vals, slot_dots, AUX_COEF * num_exp * exp_frac, float(tok_all))
        d_log16 = d_logits.astype(jnp.bfloat16)
        d_norm = jnp.einsum('lte,lde->ltd', d_log16, w_router, preferred_element_type=jnp.float32).astype(jnp.bfloat16)
        part_grad = jnp.einsum('ltd,lte->lde', u_norm, d_log16, preferred_element_type=jnp.float32)
        d_router = lax.psum(part_grad, 'dp')
        total_loss = lax.psum(main_part, 'dp') + aux_total
        return total_loss, d_router, d_norm

    tok_spec = P(None, 'dp', None)
    return jax.shard_map(local_step, mesh=mesh, in_specs=(tok_spec, tok_spec, P(None, 'dp', None, None), tok_spec, P()), out_specs=(P(), P(), tok_spec), check_vma=False)
```

profile of v0, /device:TPU:0, one launch (start us, length us, event | category | flops | bytes accessed | tf_op | source)
XLA Modules:
  0.0 276.5 jit_solution(13383112054604509439)
XLA Ops:
  7.2 0.0 copy-start
  7.2 0.0 copy-start.1
  7.2 0.0 all-reduce.3.cloned.1.call-start
  7.2 1.5 copy-done
  8.8 5.6 %fusion.30 = f32[16,64,16]{1,2,0:T(8,128)S(1)} fusion(bf16[16,64,4096]{2,1,0:T(8,128)(2,1)} %param.5, bf16[16,4096,16]{1,2,0:T(8,128)(2,1)S(1)} %copy-done), kind=kOutput, calls=%fused_computation.41 | convolution fusion | flops 134217728 | bytes 10551296 | tf_op jit(solution)/shard_map/ltd,lde->lte/dot_general | solution.py:12
  14.4 0.2 fusion.29
  14.6 0.0 copy-done.1
  14.6 0.1 select_reduce_fusion.1
  14.7 56.1 %fusion.3 = f32[16,64,1,2]{3,2,1,0:T(1,128)S(1)} fusion(bf16[16,64,2,4096]{3,2,1,0:T(2,128)(2,1)} %param.7, bf16[16,64,4096,1]{2,1,0,3:T(8,128)(2,1)} %bitcast.18), kind=kOutput, calls=%fused_computation.3 | convolution fusion | flops 16777216 | bytes 25174016 | tf_op jit(solution)/shard_map/ltkd,ltd->ltk/dot_general | solution.py:16
  70.9 0.3 copy.18
  71.2 0.6 multiply_reduce_fusion.1
  71.9 0.1 select_reduce_fusion
  72.0 0.1 pad_maximum_fusion
  72.1 42.1 %all-reduce = (f32[]{:T(128)}, f32[16,32]{1,0:T(8,128)S(1)}) all-reduce(f32[]{:T(128)} %get-tuple-element.4, f32[16,32]{1,0:T(8,128)S(1)} %pad_maximum_fusion), channel_id=1, replica_groups=mesh['dp'=32] {'dp'}, use_global_device_ids=true, to_apply=%region_4.0 | all-reduce | flops 513 | bytes 4104 | tf_op jit(solution)/shard_map/psum | solution.py:47
  114.2 0.7 slice_multiply_fusion.1
  114.8 6.7 %convolution_bitcast_fusion = f32[16,4096,16]{1,2,0:T(8,128)} fusion(bf16[16,64,4096]{2,1,0:T(8,128)(2,1)} %param.5, f32[16,64,16]{1,2,0:T(8,128)S(1)} %get-tuple-element.5, f32[16,64,16]{1,2,0:T(8,128)S(1)} %get-tuple-element.12, f32[16,16]{1,0:T(8,128)S(1)} %get-tuple-element.9), kind=kOutput, calls=%fused_computation.6 | convolution fusion | flops 134300688 | bytes 12715008 | tf_op jit(solution)/shard_map/ltd,lte->lde/dot_general | solution.py:45
  121.5 0.0 all-reduce.3.cloned.1.call-update
  122.8 5.7 %convolution_convert_fusion = bf16[16,64,4096]{2,1,0:T(8,128)(2,1)} fusion(bf16[16,4096,16]{1,2,0:T(8,128)(2,1)S(1)} %copy-done, f32[16,64,16]{1,2,0:T(8,128)S(1)} %get-tuple-element.5, f32[16,64,16]{1,2,0:T(8,128)S(1)} %get-tuple-element.12, f32[16,16]{1,0:T(8,128)S(1)} %get-tuple-element.9), kind=kOutput, calls=%fused_computation.5 | convolution fusion | flops 138494992 | bytes 10617856 | tf_op jit(solution)/shard_map/lte,lde->ltd/dot_general | solution.py:44
  128.6 135.4 %all-reduce.3.cloned.1.call-done = f32[16,4096,16]{1,2,0:T(8,128)} async-done(((f32[16,4096,16]{1,2,0:T(8,128)}), f32[16,4096,16]{1,2,0:T(8,128)}) %all-reduce.3.cloned.1.call-update) | async-done | bytes 4194320 | tf_op jit(solution)/shard_map/psum | solution.py:46
  263.9 4.7 %copy.36 = f32[16,4096,16]{1,2,0:T(8,128)} copy(f32[16,4096,16]{1,2,0:T(8,128)} %all-reduce.3.cloned.1.call-done) | data formatting | bytes 8388608
  (4 shorter events, 0.1 us)
Async XLA Ops:
  7.2 1.6 copy-start
  7.2 7.4 %copy-start.1 = (s32[16,64,2]{1,2,0:T(2,128)S(1)}, s32[16,64,2]{1,2,0:T(2,128)}, u32[]{:S(2)}) copy-start(s32[16,64,2]{1,2,0:T(2,128)} %param.6) | copy-start | bytes 24580
  7.2 256.7 %all-reduce.3.cloned.1.call-start = ((), (), s32[]{:S(2)}) async-start(), calls=%async_computation | async-start | bytes 8388608 | tf_op jit(solution)/shard_map/psum | solution.py:46
Sparse Core Ops, SparseCore 0:
  121.7 142.2 all-reduce.2
where the time goes:
time: 277 us
  waiting for transfers between devices  135 us (49%)
  matrix products  74.2 us (27%)
  blocking collectives  42.1 us (15%)
  between operations  16.5 us (6%)
  local copies, waits for them, and re-layouts  6.52 us (2%)
    psum x1, waiting for transfers between devices, local_step(): d_router = lax.psum(part_grad, 'dp')  135 us
    dot_general x1, matrix products, router_forward(): jnp.einsum('ltkd,ltd->ltk', expert_out, d_out, preferred_element_type=jnp...  56.1 us
    psum x1, blocking collectives, local_step(): total_loss = lax.psum(main_part, 'dp') + aux_total  42.1 us
    dot_general x1, matrix products, local_step(): jnp.einsum('ltd,lte->lde', u_norm, d_log16, preferred_element_type=jnp.fl...  6.68 us
    unnamed x5, local copies, waits for them, and re-layouts  6.19 us
    dot_general x1, matrix products, local_step(): jnp.einsum('lte,lde->ltd', d_log16, w_router, preferred_element_type=jnp....  5.72 us
    dot_general x1, matrix products, router_forward(): jnp.einsum('ltd,lde->lte', u_norm, w_router, preferred_element_type=jnp.f...  5.65 us
  transfers between devices with their start and end apart: 1, of which 1 were waited for; matrix products, arithmetic and copies ran while one was open for 2% of the time, Pallas kernels for 0%

commit v1 on v0

v1 whole, which is shorter than its diff:
```python
import functools

import jax
import jax.numpy as jnp
from jax import lax
from jax.experimental import pallas as pl
from jax.experimental.pallas import tpu as pltpu
from jax.sharding import PartitionSpec as P

AUX_COEF = 0.02
MESH = pl.DeviceIdType.MESH
F_STRIDE = 72
SLOTS = 4
LAG_B = 11
LAG_R0, LAG_R1, LAG_R2, LAG_R3, LAG_G3, LAG_G2, LAG_G1, LAG_G0 = 1, 2, 2, 3, 3, 2, 2, 2


def ring_kernel(dims, idx_ref, u_hbm, w_hbm, e_hbm, d_hbm, out_ref, g_ref, loss_ref,
                u_all, w_all, e_buf, d_buf, wide, p_all, a_all, part, r0, r1, r2, r3,
                cnt_src, cnt_buf, loss_src, loss_buf, loss_acc, pull_row,
                u_sem, w_sem, e_sem, d_sem, s0, v0, s1, v1, s2, v2, s3, v3, sg3, vg3, sg2, vg2, sg1, vg1, sg0, vg0,
                cs, cv, ls, lv):
    layers, toks, num_exp, depth, top_k, group = dims
    half = depth // 2
    quart = depth // 4
    piece = depth // 16
    me = lax.axis_index('dp')
    core = lax.rem(me, 2)
    px = lax.rem(lax.div(me, 2), 2)
    py = lax.rem(lax.div(me, 4), 2)
    pz = lax.div(me, 8)
    tok_all = toks * group

    def fetch_u(l):
        return (pltpu.make_async_copy(u_hbm.at[l], u_all.at[l], u_sem.at[l]),
                pltpu.make_async_copy(w_hbm.at[l], w_all.at[l], w_sem.at[l]))

    def fetch_e(l):
        slot = lax.rem(l, SLOTS)
        return (pltpu.make_async_copy(e_hbm.at[l], e_buf.at[slot], e_sem.at[slot]),
                pltpu.make_async_copy(d_hbm.at[l], d_buf.at[slot], d_sem.at[slot]))

    for l in range(SLOTS):
        for copy in fetch_u(l) + fetch_e(l):
            copy.start()

    barrier = pltpu.get_barrier_semaphore()

    def greet(p, carry):
        pl.semaphore_signal(barrier, inc=1, device_id=(lax.rem(me + p, group),), device_id_type=MESH)
        return carry
    lax.fori_loop(1, group, greet, 0)

    ids = [idx_ref[:, k, :] for k in range(top_k)]
    rows = []
    for e in range(num_exp):
        hit = jnp.where(ids[0] == e, 1.0, 0.0)
        for k in range(1, top_k):
            hit = hit + jnp.where(ids[k] == e, 1.0, 0.0)
        rows.append(hit)
    hits = jnp.concatenate(rows, axis=0).astype(jnp.bfloat16)
    cnt = lax.dot_general(jnp.ones((8, toks), jnp.bfloat16), hits, (((1,), (1,)), ((), ())),
                          preferred_element_type=jnp.float32)
    cnt_src[...] = cnt[0:1]
    cnt_buf[me] = cnt[0:1]
    loss_acc[...] = jnp.zeros_like(loss_acc)

    pl.semaphore_wait(barrier, group - 1)

    def count_copy(p, dst_slot):
        return pltpu.make_async_remote_copy(
            src_ref=cnt_src, dst_ref=cnt_buf.at[dst_slot], send_sem=cs.at[p], recv_sem=cv.at[p],
            device_id=(lax.rem(me + p, group),), device_id_type=MESH)

    def loss_copy(p, dst_slot):
        return pltpu.make_async_remote_copy(
            src_ref=loss_src, dst_ref=loss_buf.at[dst_slot], send_sem=ls.at[p], recv_sem=lv.at[p],
            device_id=(lax.rem(me + p, group),), device_id_type=MESH)

    def send_counts(p, carry):
        count_copy(p, me).start()
        return carry
    lax.fori_loop(1, group, send_counts, 0)

    def forward(l):
        slot = lax.rem(l, SLOTS)
        for copy in fetch_u(l):
            copy.wait()
        logits = lax.dot_general(w_all[l], u_all[l], (((1,), (1,)), ((), ())), preferred_element_type=jnp.float32)
        for copy in fetch_e(l):
            copy.wait()
        accs = [[], []]
        tiles = depth // 128
        for tb in range(toks // 8):
            for t in range(8):
                tok = tb * 8 + t
                wide[pl.ds(tok * F_STRIDE, 2 * tiles), :] = (
                    e_buf[slot, pl.ds(tok * 2 * tiles, 2 * tiles), :].astype(jnp.float32))
            dy = d_buf[slot, pl.ds(tb * 8 * tiles, 8 * tiles), :].astype(jnp.float32)
            sums = [[None, None], [None, None]]
            for j in range(tiles):
                for k in range(2):
                    ev = wide[pl.ds(tb * 8 * F_STRIDE + 2 * j + k, 8, stride=F_STRIDE), :]
                    prod = ev * dy[8 * j:8 * j + 8]
                    old = sums[k][j % 2]
                    sums[k][j % 2] = prod if old is None else old + prod
            for k in range(2):
                accs[k].append(sums[k][0] + sums[k][1])

        @pl.when(l + SLOTS < layers)
        def _():
            for copy in fetch_u(l + SLOTS) + fetch_e(l + SLOTS):
                copy.start()

        dots = jnp.sum(jnp.concatenate(accs[0] + accs[1], axis=0).T, axis=0, keepdims=True)
        dot0, dot1 = dots[:, :toks], dots[:, toks:]
        row_id = lax.broadcasted_iota(jnp.int32, (num_exp, toks), 0)
        pair = idx_ref[l]
        sel0 = row_id == pair[0:1]
        sel1 = row_id == pair[1:2]
        top = jnp.max(logits, axis=0, keepdims=True)
        ex = jnp.exp(logits - top)
        p_all[l] = ex / jnp.sum(ex, axis=0, keepdims=True)
        c0 = jnp.sum(jnp.where(sel0, logits, 0.0), axis=0, keepdims=True)
        c1 = jnp.sum(jnp.where(sel1, logits, 0.0), axis=0, keepdims=True)
        cm = jnp.maximum(c0, c1)
        x0, x1 = jnp.exp(c0 - cm), jnp.exp(c1 - cm)
        xs = x0 + x1
        g0, g1 = x0 / xs, x1 / xs
        inner = g0 * dot0 + g1 * dot1
        loss_acc[0:1, :] += inner
        scale = float(tok_all)
        dc0 = g0 * (scale * dot0 - scale * inner)
        dc1 = g1 * (scale * dot1 - scale * inner)
        a_all[l] = jnp.where(sel0, dc0, 0.0) + jnp.where(sel1, dc1, 0.0)

    def get_counts():
        def one(p, carry):
            count_copy(p, lax.rem(me + group - p, group)).wait_recv()
            return carry
        lax.fori_loop(1, group, one, 0)
        pull_row[...] = jnp.sum(cnt_buf[...], axis=0) * (AUX_COEF * num_exp / (top_k * tok_all))

    def halves(l):
        odd = lax.rem(l, 2)
        a1 = jnp.where(odd == 0, px, py)
        a2 = jnp.where(odd == 0, py, px)
        step1 = jnp.where(odd == 0, 2, 4)
        step2 = jnp.where(odd == 0, 4, 2)
        peer1 = me + step1 * (1 - 2 * a1)
        peer2 = me + step2 * (1 - 2 * a2)
        return a1, a2, peer1, peer2

    partner = me + 1 - 2 * core

    def lanes(start, size):
        return pl.ds(pl.multiple_of(start, piece), size)

    def remote(src, dst, ss, rs, dev):
        return pltpu.make_async_remote_copy(src_ref=src, dst_ref=dst, send_sem=ss, recv_sem=rs,
                                            device_id=(dev,), device_id_type=MESH)

    def copy_r0(l):
        return [remote(part.at[l, 1 - core], r0.at[l], s0.at[l], v0.at[l], partner)]

    def copy_r1(l):
        a1, a2, peer1, peer2 = halves(l)
        return [remote(part.at[l, core, :, lanes(half * (1 - a1), half)], r1.at[l], s1.at[l], v1.at[l], peer1)]

    def copy_r2(l):
        a1, a2, peer1, peer2 = halves(l)
        return [remote(part.at[l, core, :, lanes(half * a1 + quart * (1 - a2), quart)], r2.at[l], s2.at[l], v2.at[l],
                       peer2)]

    def copy_r3(l):
        a1, a2, peer1, peer2 = halves(l)
        out = []
        for dz in range(1, 4):
            zt = lax.rem(pz + dz, 4)
            out.append(remote(part.at[l, core, :, lanes(half * a1 + quart * a2 + piece * zt, piece)],
                              r3.at[l, dz - 1], s3.at[l, dz - 1], v3.at[l, dz - 1], me + 8 * (zt - pz)))
        return out

    def copy_g3(l, receive=False):
        a1, a2, peer1, peer2 = halves(l)
        out = []
        for dz in range(1, 4):
            zt = lax.rem(pz + dz, 4)
            zo = lax.rem(pz + 4 - dz, 4) if receive else pz
            ref = out_ref.at[l, core, :, lanes(half * a1 + quart * a2 + piece * zo, piece)]
            out.append(remote(ref, ref, sg3.at[l, dz - 1], vg3.at[l, dz - 1], me + 8 * (zt - pz)))
        return out

    def copy_g2(l, receive=False):
        a1, a2, peer1, peer2 = halves(l)
        own = 1 - a2 if receive else a2
        ref = out_ref.at[l, core, :, lanes(half * a1 + quart * own, quart)]
        return [remote(ref, ref, sg2.at[l], vg2.at[l], peer2)]

    def copy_g1(l, receive=False):
        a1, a2, peer1, peer2 = halves(l)
        own = 1 - a1 if receive else a1
        ref = out_ref.at[l, core, :, lanes(half * own, half)]
        return [remote(ref, ref, sg1.at[l], vg1.at[l], peer1)]

    def copy_g0(l, receive=False):
        own = 1 - core if receive else core
        ref = out_ref.at[l, own]
        return [remote(ref, ref, sg0.at[l], vg0.at[l], partner)]

    def start(copies):
        for copy in copies:
            copy.start()

    def landed(copies):
        for copy in copies:
            copy.wait_recv()

    def sent(copies):
        for copy in copies:
            copy.wait_send()

    def backward(l):
        at = lax.broadcasted_iota(jnp.int32, (num_exp, num_exp * layers), 1)
        row = lax.broadcasted_iota(jnp.int32, (num_exp, num_exp * layers), 0)
        pull = jnp.sum(jnp.where(at == layers * row + l, pull_row[...], 0.0), axis=1, keepdims=True)
        prob = p_all[l]
        inner = jnp.sum(prob * pull, axis=0, keepdims=True)
        loss_acc[1:2, :] += inner
        grad = (a_all[l] + prob * (pull - inner)).astype(jnp.bfloat16)
        g_ref[l] = grad
        dw = jnp.dot(grad, u_all[l], preferred_element_type=jnp.float32)
        part[l, 0] = dw[:8]
        part[l, 1] = dw[8:]
        start(copy_r0(l))

        @pl.when(l == layers - 1)
        def _():
            total = loss_acc[0:1, :] + loss_acc[1:2, :] * (1.0 / tok_all)
            mine = jnp.broadcast_to(jnp.sum(total, axis=1, keepdims=True), (1, 128))
            loss_src[...] = mine
            loss_buf[me] = mine

            def send_loss(p, carry):
                loss_copy(p, me).start()
                return carry
            lax.fori_loop(1, group, send_loss, 0)

    def stage_r0(l):
        a1, a2, peer1, peer2 = halves(l)
        landed(copy_r0(l))
        away = lanes(half * (1 - a1), half)
        part[l, core, :, away] += r0[l, :, away]
        start(copy_r1(l))
        keep = lanes(half * a1, half)
        part[l, core, :, keep] += r0[l, :, keep]

    def stage_r1(l):
        a1, a2, peer1, peer2 = halves(l)
        landed(copy_r1(l))
        away = lanes(half * a1 + quart * (1 - a2), quart)
        part[l, core, :, away] += r1[l, :, lanes(quart * (1 - a2), quart)]
        start(copy_r2(l))
        keep = lanes(half * a1 + quart * a2, quart)
        part[l, core, :, keep] += r1[l, :, lanes(quart * a2, quart)]

    def stage_r2(l):
        a1, a2, peer1, peer2 = halves(l)
        landed(copy_r2(l))
        keep = lanes(half * a1 + quart * a2, quart)
        part[l, core, :, keep] += r2[l]
        start(copy_r3(l))

    def stage_r3(l):
        a1, a2, peer1, peer2 = halves(l)
        landed(copy_r3(l))
        keep = lanes(half * a1 + quart * a2 + piece * pz, piece)
        out_ref[l, core, :, keep] = (part[l, core, :, keep] + r3[l, 0]) + (r3[l, 1] + r3[l, 2])
        start(copy_g3(l))

    def stage_g3(l):
        landed(copy_g3(l, True))
        start(copy_g2(l))

    def stage_g2(l):
        landed(copy_g2(l, True))
        start(copy_g1(l))

    def stage_g1(l):
        landed(copy_g1(l, True))
        start(copy_g0(l))

    def stage_g0(l):
        landed(copy_g0(l, True))
        sent(copy_r0(l) + copy_r1(l) + copy_r2(l) + copy_r3(l) + copy_g3(l) + copy_g2(l) + copy_g1(l) + copy_g0(l))

    stages = [(0, forward), (LAG_B, backward)]
    lag = LAG_B
    for add, stage in ((LAG_R0, stage_r0), (LAG_R1, stage_r1), (LAG_R2, stage_r2), (LAG_R3, stage_r3),
                       (LAG_G3, stage_g3), (LAG_G2, stage_g2), (LAG_G1, stage_g1), (LAG_G0, stage_g0)):
        lag += add
        stages.append((lag, stage))

    def step(s, carry):
        @pl.when(s == LAG_B)
        def _():
            get_counts()
        for delay, stage in stages:
            @pl.when(jnp.logical_and(s >= delay, s < delay + layers))
            def _():
                stage(s - delay)
        return carry
    lax.fori_loop(0, layers + lag, step, 0)

    def finish(p, carry):
        count_copy(p, me).wait_send()
        loss_copy(p, me).wait_send()
        loss_copy(p, lax.rem(me + group - p, group)).wait_recv()
        return carry
    lax.fori_loop(1, group, finish, 0)
    loss_ref[...] = jnp.sum(loss_buf[...], axis=0)


def norm_kernel(layers_step, g_ref, w_ref, dr_ref, dn_ref, dr_out, sem):
    step = pl.program_id(0)
    move = pltpu.make_async_copy(dr_ref, dr_out, sem)

    @pl.when(step == 0)
    def _():
        move.start()

    for i in range(layers_step):
        dn_ref[i] = lax.dot_general(g_ref[i], w_ref[i], (((0,), (0,)), ((), ())),
                                    preferred_element_type=jnp.float32).astype(jnp.bfloat16)

    @pl.when(step == pl.num_programs(0) - 1)
    def _():
        move.wait()


def solution(mesh):
    group = mesh.shape['dp']

    def local_step(u_norm, expert_idx, expert_out, d_out, w_router):
        layers, toks, depth = u_norm.shape
        num_exp = w_router.shape[2]
        top_k = expert_idx.shape[2]
        tiles = depth // 128
        idx_t = expert_idx.transpose(0, 2, 1)
        w_t = w_router.transpose(0, 2, 1)
        e_rows = expert_out.reshape(layers, toks, top_k, tiles, 128).transpose(0, 1, 3, 2, 4)
        e_rows = e_rows.reshape(layers, toks * tiles * top_k, 128)
        d_rows = d_out.reshape(layers, toks // 8, 8, tiles, 128).transpose(0, 1, 3, 2, 4)
        d_rows = d_rows.reshape(layers, toks * tiles, 128)
        f32, bf16 = jnp.float32, jnp.bfloat16
        dma = pltpu.SemaphoreType.DMA
        vmem = pl.BlockSpec(memory_space=pltpu.VMEM)
        hbm = pl.BlockSpec(memory_space=pltpu.HBM)
        dims = (layers, toks, num_exp, depth, top_k, group)
        scratch = [
            pltpu.VMEM((layers, toks, depth), bf16), pltpu.VMEM((layers, num_exp, depth), bf16),
            pltpu.VMEM((SLOTS, toks * tiles * top_k, 128), bf16), pltpu.VMEM((SLOTS, toks * tiles, 128), bf16),
            pltpu.VMEM((toks * F_STRIDE, 128), f32),
            pltpu.VMEM((layers, num_exp, toks), f32), pltpu.VMEM((layers, num_exp, toks), f32),
            pltpu.VMEM((layers, 2, 8, depth), f32), pltpu.VMEM((layers, 8, depth), f32),
            pltpu.VMEM((layers, 8, depth // 2), f32), pltpu.VMEM((layers, 8, depth // 4), f32),
            pltpu.VMEM((layers, 3, 8, depth // 16), f32),
            pltpu.VMEM((1, num_exp * layers), f32), pltpu.VMEM((group, 1, num_exp * layers), f32),
            pltpu.VMEM((1, 128), f32), pltpu.VMEM((group, 1, 128), f32), pltpu.VMEM((8, toks), f32),
            pltpu.VMEM((1, num_exp * layers), f32),
            dma((layers,)), dma((layers,)), dma((SLOTS,)), dma((SLOTS,)),
            dma((layers,)), dma((layers,)), dma((layers,)), dma((layers,)), dma((layers,)), dma((layers,)),
            dma((layers, 3)), dma((layers, 3)), dma((layers, 3)), dma((layers, 3)),
            dma((layers,)), dma((layers,)), dma((layers,)), dma((layers,)), dma((layers,)), dma((layers,)),
            dma((group,)), dma((group,)), dma((group,)), dma((group,)),
        ]
        d_router, grads, loss = pl.pallas_call(
            functools.partial(ring_kernel, dims),
            out_shape=(jax.ShapeDtypeStruct((layers, 2, 8, depth), f32),
                       jax.ShapeDtypeStruct((layers, num_exp, toks), bf16),
                       jax.ShapeDtypeStruct((1, 128), f32)),
            in_specs=[vmem, hbm, hbm, hbm, hbm],
            out_specs=(vmem, vmem, vmem),
            scratch_shapes=scratch,
            compiler_params=pltpu.CompilerParams(collective_id=0, has_side_effects=True,
                                                 vmem_limit_bytes=48 * 1024 * 1024),
            name='ring',
        )(idx_t, u_norm, w_t, e_rows, d_rows)

        per = 4
        d_norm, d_router = pl.pallas_call(
            functools.partial(norm_kernel, per),
            grid=(layers // per,),
            out_shape=(jax.ShapeDtypeStruct((layers, toks, depth), bf16),
                       jax.ShapeDtypeStruct((layers, 2, 8, depth), f32)),
            in_specs=[pl.BlockSpec((per, num_exp, toks), lambda i: (i, 0, 0)),
                      pl.BlockSpec((per, num_exp, depth), lambda i: (i, 0, 0)),
                      pl.BlockSpec(memory_space=pl.ANY)],
            out_specs=(pl.BlockSpec((per, toks, depth), lambda i: (i, 0, 0)),
                       pl.BlockSpec(memory_space=pltpu.HBM)),
            scratch_shapes=[dma(())],
            name='norm',
        )(grads, w_t, d_router)
        d_router = d_router.reshape(layers, num_exp, depth).transpose(0, 2, 1)
        return loss[0, 0], d_router, d_norm

    tok_spec = P(None, 'dp', None)
    return jax.shard_map(local_step, mesh=mesh,
                         in_specs=(tok_spec, tok_spec, P(None, 'dp', None, None), tok_spec, P()),
                         out_specs=(P(), P(), tok_spec), check_vma=False)
```

time: 277 us -> 215 us (0.78)
  Pallas kernels: 0 us -> 209 us
  waiting for transfers between devices: 135 us -> 0 us
  matrix products: 74.2 us -> 0 us
  blocking collectives: 42.1 us -> 0 us
  between operations: 16.5 us -> 1.82 us
  local copies, waits for them, and re-layouts: 6.52 us -> 2.92 us
    pallas_call x0 -> x2, Pallas kernels: none -> 209 us  [the longest x1 131 us: local_step(): pl.pallas_call(functools.partial(norm_kernel, per), grid=(layers // per,)...]
    psum x1 -> x0, waiting for transfers between devices: 135 us -> none  [local_step(): d_router = lax.psum(part_grad, 'dp')]
    dot_general x4 -> x0, matrix products: 74.2 us -> none  [the longest x1 56.1 us: router_forward(): jnp.einsum('ltkd,ltd->ltk', expert_out, d_out, preferred_element_type=jnp...]
    psum x1 -> x0, blocking collectives: 42.1 us -> none  [local_step(): total_loss = lax.psum(main_part, 'dp') + aux_total]
    unnamed x5 -> x6, local copies, waits for them, and re-layouts: 6.19 us -> 2.92 us
  transfers between devices with their start and end apart: 1 -> 0, of which waited for: 1 -> 0; matrix products, arithmetic and copies ran while one was open for 2% -> 0% of each run, Pallas kernels for 0% -> 0%
where the time goes in v1:
time: 215 us; the launch traced here: 214 us
  Pallas kernels  209 us (97%)
  local copies, waits for them, and re-layouts  2.92 us (1%)
    pallas_call x1, Pallas kernels, local_step(): pl.pallas_call(functools.partial(norm_kernel, per), grid=(layers // per,)...  131 us
    pallas_call x1, Pallas kernels, local_step(): pl.pallas_call(functools.partial(ring_kernel, dims), out_shape=(jax.Shape...  78.9 us

profile of v1, /device:TPU:0, one launch (start us, length us, event | category | flops | bytes accessed | tf_op | source)
XLA Modules:
  0.0 214.2 jit_solution(12330580463729193564)
XLA Ops:
  0.6 0.0 copy-start
  0.6 1.6 copy-done
  2.2 0.0 copy-start.2
  2.2 0.7 copy-done.2
  2.9 78.9 %ring.1 = (f32[16,2,8,4096]{3,2,1,0:T(8,128)}, bf16[16,16,64]{2,1,0:T(8,128)(2,1)S(1)}, f32[1,128]{1,0:T(1,128)S(1)}) custom-call(s32[16,2,64]{2,1,0:T(2,128)S(1)} %bitcast.19, bf16[16,64,4096]{2,1,0:T(8,128)(2,1)} %u_hbm.1, bf16[16,16,4096]{2,1,0:T(8,128)(2,1)S(1)} %bitcast.18, bf16[16,4096,128]{2,1,0:T(8,128)(2,1)} %bitcast.21, bf16[16,2048,128]{2,1,0:T(8,128)(2,1)} %bitcast.22), custom_call_target="tpu_custom_call" | custom-call | tf_op jit(solution)/shard_map/ring/pallas_call | solution.py:377
  81.8 0.0 copy-start.1
  81.8 0.6 copy-done.1
  82.5 130.5 %norm.1 = (bf16[16,64,4096]{2,1,0:T(8,128)(2,1)}, f32[16,2,8,4096]{3,2,1,0:T(8,128)}) custom-call(bf16[16,16,64]{2,1,0:T(8,128)(2,1)} %copy-done.1, bf16[16,16,4096]{2,1,0:T(8,128)(2,1)} %bitcast.17, f32[16,2,8,4096]{3,2,1,0:T(8,128)} %get-tuple-element.10.dr_ref), custom_call_target="tpu_custom_call" | custom-call | tf_op jit(solution)/shard_map/norm/pallas_call | solution.py:391
Async XLA Ops:
  0.6 1.6 copy-start
  2.2 0.7 copy-start.2
  81.8 0.6 copy-start.1

commit v2 on v0

v2 whole, which is shorter than its diff:
```python
import functools

import jax
import jax.numpy as jnp
from jax import lax
from jax.experimental import pallas as pl
from jax.experimental.pallas import tpu as pltpu
from jax.sharding import PartitionSpec as P

AUX_COEF = 0.02
MESH = pl.DeviceIdType.MESH
F_STRIDE = 73
SLOTS = 6
GREET = 2
BITS = {'c': 1, 'x': 2, 'y': 4, 'p': 8, 'q': 16}
ORDERS = ('xpyq', 'ypxq') * 8
T_START, T_FWD, T_BWD, T_COUNTS = 1.5, 0.85, 0.5, 12.5
T_STAGE = (0.1, 0.08, 0.06, 0.05, 0.05, 0.04, 0.04, 0.04, 0.04, 0.03)
DELAY = {'c': 1.5, 'x': 3.0, 'y': 3.0, 'p': 3.0, 'q': 3.5}
AHEAD = 1.5
PRIO = 3


def plan_order(orders):
    layers = len(orders)
    paths = ['c' + o + o[::-1] + 'c' for o in orders]
    sizes = [2.8 / 2 ** i for i in range(5)]
    sizes = sizes + sizes[::-1]
    link = dict.fromkeys('cxypm', 0.0)
    arrive, plan = {}, []
    now, done_f, done_b = T_START, 0, 0

    def send(i, l):
        axis, cost = paths[l][i], sizes[i]
        if axis == 'c':
            cost = cost * 0.08
        lane = 'p' if axis == 'q' else axis
        link[lane] = max(now, link[lane]) + cost
        end = link[lane]
        if axis == 'q':
            link['m'] = max(end - cost, link['m']) + 2 * cost
            end = max(end, link['m'])
        arrive[i, l] = end + DELAY[axis]

    counts = False
    while True:
        ready = [k for k, v in arrive.items() if v <= now]
        first = paths[min(done_b, layers - 1)][1]
        if ready:
            if PRIO == 3:
                i, l = min(ready, key=lambda k: (-k[0], k[1]))
            elif PRIO == 0:
                i, l = min(ready)
            elif PRIO == 1:
                i, l = min(ready, key=lambda k: (k[1], k[0]))
            else:
                i, l = min(ready, key=lambda k: arrive[k])
            del arrive[i, l]
            now += T_STAGE[i]
            plan.append((i, l))
            if i < 9:
                send(i + 1, l)
        elif done_b < done_f and now >= T_COUNTS and (link[first] - now < AHEAD or not arrive):
            now += T_BWD
            if not counts:
                plan.append(('counts', 0))
                counts = True
            plan.append(('backward', done_b))
            send(0, done_b)
            done_b += 1
        elif done_f < layers:
            now += T_FWD
            plan.append(('forward', done_f))
            done_f += 1
        elif now < T_COUNTS:
            now = T_COUNTS
        elif arrive:
            now = min(arrive.values())
            if done_b < layers:
                now = min(now, max(link[first] - AHEAD + 0.01, now if now < min(arrive.values()) else 0))
                now = max(now, min(min(arrive.values()), link[first] - AHEAD + 0.01))
        else:
            return plan


def ring_kernel(dims, idx_hbm, u_hbm, w_hbm, e_hbm, d_hbm, out_ref, g_ref, loss_ref,
                idx_ref, u_all, w_all, e_buf, d_buf, wide, p_all, a_all, part, r0, r1, r2, r3, r4,
                cnt_src, cnt_buf, loss_src, loss_buf, loss_acc, pull_row,
                i_sem, u_sem, w_sem, e_sem, d_sem, *sems):
    layers, toks, num_exp, depth, top_k, group = dims
    send_sems, recv_sems = sems[:10], sems[10:20]
    cs, cv, ls, lv = sems[20:]
    landing = (r0, r1, r2, r3, r4)
    piece = depth // 16
    me = lax.axis_index('dp')
    bit = {axis: lax.rem(lax.div(me, step), 2) for axis, step in BITS.items()}
    peer = {axis: me + step * (1 - 2 * bit[axis]) for axis, step in BITS.items()}
    core = bit['c']
    tok_all = toks * group

    barrier = pltpu.get_barrier_semaphore()

    def greet(p, carry):
        pl.semaphore_signal(barrier, inc=1, device_id=(lax.rem(me + p, group),), device_id_type=MESH)
        return carry
    lax.fori_loop(1, group, greet, 0)

    def fetch(l):
        slot = lax.rem(l, SLOTS)
        return (pltpu.make_async_copy(u_hbm.at[l], u_all.at[l], u_sem.at[slot]),
                pltpu.make_async_copy(w_hbm.at[l], w_all.at[l], w_sem.at[slot]),
                pltpu.make_async_copy(e_hbm.at[l], e_buf.at[slot], e_sem.at[slot]),
                pltpu.make_async_copy(d_hbm.at[l], d_buf.at[slot], d_sem.at[slot]))

    get_idx = pltpu.make_async_copy(idx_hbm, idx_ref, i_sem)
    get_idx.start()
    for l in range(SLOTS):
        for copy in fetch(l):
            copy.start()
    loss_acc[...] = jnp.zeros_like(loss_acc)
    get_idx.wait()

    ids = [idx_ref[:, k, :] for k in range(top_k)]
    rows = []
    for e in range(num_exp):
        hit = jnp.where(ids[0] == e, 1.0, 0.0)
        for k in range(1, top_k):
            hit = hit + jnp.where(ids[k] == e, 1.0, 0.0)
        rows.append(hit)
    hits = jnp.concatenate(rows, axis=0).astype(jnp.bfloat16)
    cnt = lax.dot_general(jnp.ones((8, toks), jnp.bfloat16), hits, (((1,), (1,)), ((), ())),
                          preferred_element_type=jnp.float32)
    cnt_src[...] = cnt[0:1]
    cnt_buf[me] = cnt[0:1]

    def everyone(src, buf, ss, rs):
        def one(p, carry):
            pltpu.make_async_remote_copy(src_ref=src, dst_ref=buf.at[me], send_sem=ss, recv_sem=rs,
                                         device_id=(lax.rem(me + p, group),), device_id_type=MESH).start()
            return carry
        lax.fori_loop(1, group, one, 0)

    def drain(ref, sem):
        pltpu.make_async_copy(ref, ref, sem).wait()

    def forward(l):
        slot = lax.rem(l, SLOTS)
        for copy in fetch(l):
            copy.wait()
        logits = lax.dot_general(w_all[l], u_all[l], (((1,), (1,)), ((), ())), preferred_element_type=jnp.float32)
        accs = [[], []]
        tiles = depth // 128
        for tb in range(toks // 8):
            for t in range(8):
                tok = tb * 8 + t
                wide[pl.ds(tok * F_STRIDE, 2 * tiles), :] = (
                    e_buf[slot, pl.ds(tok * 2 * tiles, 2 * tiles), :].astype(jnp.float32))
            sums = [[None, None], [None, None]]
            for j in range(tiles):
                if j % 2 == 0:
                    dy = d_buf[slot, pl.ds((tb * tiles + j) * 8, 16), :].astype(jnp.float32)
                for k in range(2):
                    ev = wide[pl.ds(tb * 8 * F_STRIDE + 2 * j + k, 8, stride=F_STRIDE), :]
                    prod = ev * (dy[:8] if j % 2 == 0 else dy[8:])
                    old = sums[k][j % 2]
                    sums[k][j % 2] = prod if old is None else old + prod
            for k in range(2):
                accs[k].append(sums[k][0] + sums[k][1])

        @pl.when(l + SLOTS < layers)
        def _():
            for copy in fetch(l + SLOTS):
                copy.start()

        dots = jnp.sum(jnp.concatenate(accs[0] + accs[1], axis=0).T, axis=0, keepdims=True)
        dot0, dot1 = dots[:, :toks], dots[:, toks:]
        row_id = lax.broadcasted_iota(jnp.int32, (num_exp, toks), 0)
        pair = idx_ref[l]
        sel0 = row_id == pair[0:1]
        sel1 = row_id == pair[1:2]
        top = jnp.max(logits, axis=0, keepdims=True)
        ex = jnp.exp(logits - top)
        p_all[l] = ex / jnp.sum(ex, axis=0, keepdims=True)
        c0 = jnp.sum(jnp.where(sel0, logits, 0.0), axis=0, keepdims=True)
        c1 = jnp.sum(jnp.where(sel1, logits, 0.0), axis=0, keepdims=True)
        cm = jnp.maximum(c0, c1)
        x0, x1 = jnp.exp(c0 - cm), jnp.exp(c1 - cm)
        xs = x0 + x1
        g0, g1 = x0 / xs, x1 / xs
        inner = g0 * dot0 + g1 * dot1
        loss_acc[0:1, :] += inner
        scale = float(tok_all)
        dc0 = g0 * (scale * dot0 - scale * inner)
        dc1 = g1 * (scale * dot1 - scale * inner)
        a_all[l] = jnp.where(sel0, dc0, 0.0) + jnp.where(sel1, dc1, 0.0)

    def get_counts():
        drain(cnt_buf.at[pl.ds(0, group - 1)], cv)
        pull_row[...] = jnp.sum(cnt_buf[...], axis=0) * (AUX_COEF * num_exp / (top_k * tok_all))

    kept = {}
    for order in dict.fromkeys(ORDERS):
        offs = [0]
        for i, axis in enumerate(order):
            offs.append(offs[-1] + bit[axis] * (depth >> (i + 1)))
        kept[order] = offs

    def lanes(start, size):
        return pl.ds(start if isinstance(start, int) else pl.multiple_of(start, piece), size)

    def exchange(i, l):
        order = ORDERS[l]
        axis = ('c' + order + order[::-1] + 'c')[i]
        offs = kept[order]
        if i == 0:
            src, dst = part.at[l, 1 - core], r0.at[l]
        elif i < 5:
            size = depth >> i
            src = part.at[l, core, :, lanes(offs[i - 1] + (1 - bit[axis]) * size, size)]
            dst = landing[i].at[l]
        else:
            size = depth >> (9 - i)
            src = dst = out_ref.at[l, core, :, lanes(offs[9 - i], size)]
        return pltpu.make_async_remote_copy(src_ref=src, dst_ref=dst, send_sem=send_sems[i], recv_sem=recv_sems[i].at[l],
                                            device_id=(peer[axis],), device_id_type=MESH)

    def backward(l):
        at = lax.broadcasted_iota(jnp.int32, (num_exp, num_exp * layers), 1)
        row = lax.broadcasted_iota(jnp.int32, (num_exp, num_exp * layers), 0)
        pull = jnp.sum(jnp.where(at == layers * row + l, pull_row[...], 0.0), axis=1, keepdims=True)
        prob = p_all[l]
        inner = jnp.sum(prob * pull, axis=0, keepdims=True)
        loss_acc[1:2, :] += inner
        grad = (a_all[l] + prob * (pull - inner)).astype(jnp.bfloat16)
        g_ref[l] = grad
        dw = jnp.dot(grad, u_all[l], preferred_element_type=jnp.float32)
        part[l, 0] = dw[:8]
        part[l, 1] = dw[8:]
        exchange(0, l).start()
        if l == layers - 1:
            total = loss_acc[0:1, :] + loss_acc[1:2, :] * (1.0 / tok_all)
            mine = jnp.broadcast_to(jnp.sum(total, axis=1, keepdims=True), (1, 128))
            loss_src[...] = mine
            loss_buf[me] = mine
            everyone(loss_src, loss_buf, ls, lv)

    def arrived(i, l):
        order = ORDERS[l]
        offs = kept[order]
        if i < 5:
            exchange(i, l).wait_recv()
            got = landing[i]
            if i < 4:
                size = depth >> (i + 1)
                mine = bit[order[i]]
                for side in (1 - mine, mine):
                    here = lanes(offs[i] + side * size, size)
                    part[l, core, :, here] += got[l, :, lanes(side * size, size)]
                    if side is not mine:
                        exchange(i + 1, l).start()
            else:
                here = lanes(offs[4], piece)
                out_ref[l, core, :, here] = part[l, core, :, here] + got[l]
                exchange(5, l).start()
        else:
            exchange(i, l).wait_recv()
            if i < 9:
                exchange(i + 1, l).start()

    plan = plan_order(ORDERS)
    n_fwd = 0
    at = 0
    while at < len(plan):
        kind, l = plan[at]
        if kind == 'forward':
            stop = at
            while stop < len(plan) and plan[stop][0] == 'forward':
                stop += 1
            count = stop - at
            if n_fwd == 0:
                lax.fori_loop(0, GREET, lambda s, c: (forward(s), c)[1], 0)
                pl.semaphore_wait(barrier, group - 1)
                everyone(cnt_src, cnt_buf, cs, cv)
                lax.fori_loop(GREET, count, lambda s, c: (forward(s), c)[1], 0)
            else:
                lax.fori_loop(n_fwd, n_fwd + count, lambda s, c: (forward(s), c)[1], 0)
            n_fwd += count
            at = stop
            continue
        if kind == 'counts':
            get_counts()
        elif kind == 'backward':
            backward(l)
        else:
            arrived(kind, l)
        at += 1

    drain(loss_buf.at[pl.ds(0, group - 1)], lv)
    drain(loss_buf.at[pl.ds(0, group - 1)], ls)
    drain(cnt_buf.at[pl.ds(0, group - 1)], cs)
    for i in range(10):
        drain(landing[i if i < 5 else 9 - i], send_sems[i])
    loss_ref[...] = jnp.sum(loss_buf[...], axis=0)


def norm_kernel(per, g_ref, w_ref, dr_ref, dn_hbm, dr_hbm, buf, dn_sem, dr_sem):
    layers = g_ref.shape[0]
    move = pltpu.make_async_copy(dr_ref, dr_hbm, dr_sem)
    move.start()

    def put(b):
        return pltpu.make_async_copy(buf.at[pl.ds(b * per, per)], dn_hbm.at[pl.ds(b * per, per)], dn_sem.at[b])
    for b in range(layers // per):
        for l in range(b * per, b * per + per):
            buf[l] = lax.dot_general(g_ref[l], w_ref[l], (((0,), (0,)), ((), ())),
                                     preferred_element_type=jnp.float32).astype(jnp.bfloat16)
        put(b).start()
    for b in range(layers // per):
        put(b).wait()
    move.wait()


def solution(mesh):
    group = mesh.shape['dp']

    def local_step(u_norm, expert_idx, expert_out, d_out, w_router):
        layers, toks, depth = u_norm.shape
        num_exp = w_router.shape[2]
        top_k = expert_idx.shape[2]
        tiles = depth // 128
        idx_t = expert_idx.transpose(0, 2, 1)
        w_t = w_router.transpose(0, 2, 1)
        e_rows = expert_out.reshape(layers, toks, top_k, tiles, 128).transpose(0, 1, 3, 2, 4)
        e_rows = e_rows.reshape(layers, toks * tiles * top_k, 128)
        d_rows = d_out.reshape(layers, toks // 8, 8, tiles, 128).transpose(0, 1, 3, 2, 4)
        d_rows = d_rows.reshape(layers, toks * tiles, 128)
        f32, bf16 = jnp.float32, jnp.bfloat16
        dma = pltpu.SemaphoreType.DMA
        vmem = pl.BlockSpec(memory_space=pltpu.VMEM)
        hbm = pl.BlockSpec(memory_space=pltpu.HBM)
        dims = (layers, toks, num_exp, depth, top_k, group)
        scratch = [
            pltpu.VMEM((layers, top_k, toks), jnp.int32),
            pltpu.VMEM((layers, toks, depth), bf16), pltpu.VMEM((layers, num_exp, depth), bf16),
            pltpu.VMEM((SLOTS, toks * tiles * top_k, 128), bf16), pltpu.VMEM((SLOTS, toks * tiles, 128), bf16),
            pltpu.VMEM((toks * F_STRIDE, 128), f32),
            pltpu.VMEM((layers, num_exp, toks), f32), pltpu.VMEM((layers, num_exp, toks), f32),
            pltpu.VMEM((layers, 2, 8, depth), f32), pltpu.VMEM((layers, 8, depth), f32),
            pltpu.VMEM((layers, 8, depth // 2), f32), pltpu.VMEM((layers, 8, depth // 4), f32),
            pltpu.VMEM((layers, 8, depth // 8), f32), pltpu.VMEM((layers, 8, depth // 16), f32),
            pltpu.VMEM((1, num_exp * layers), f32), pltpu.VMEM((group, 1, num_exp * layers), f32),
            pltpu.VMEM((1, 128), f32), pltpu.VMEM((group, 1, 128), f32), pltpu.VMEM((8, toks), f32),
            pltpu.VMEM((1, num_exp * layers), f32),
            dma(()), dma((SLOTS,)), dma((SLOTS,)), dma((SLOTS,)), dma((SLOTS,)),
        ] + [dma(())] * 10 + [dma((layers,))] * 10 + [dma(())] * 4
        d_router, grads, loss = pl.pallas_call(
            functools.partial(ring_kernel, dims),
            out_shape=(pltpu.VMEM((layers, 2, 8, depth), f32), pltpu.VMEM((layers, num_exp, toks), bf16),
                       pltpu.VMEM((1, 128), f32)),
            in_specs=[hbm, hbm, hbm, hbm, hbm],
            out_specs=(vmem, vmem, vmem),
            scratch_shapes=scratch,
            compiler_params=pltpu.CompilerParams(collective_id=0, has_side_effects=True,
                                                 vmem_limit_bytes=48 * 1024 * 1024),
            name='ring',
        )(pltpu.with_memory_space_constraint(idx_t, pltpu.HBM), u_norm, pltpu.with_memory_space_constraint(w_t, pltpu.HBM), e_rows, d_rows)

        per = 2
        d_norm, d_router = pl.pallas_call(
            functools.partial(norm_kernel, per),
            out_shape=(jax.ShapeDtypeStruct((layers, toks, depth), bf16),
                       jax.ShapeDtypeStruct((layers, 2, 8, depth), f32)),
            in_specs=[vmem, vmem, vmem],
            out_specs=(hbm, hbm),
            scratch_shapes=[pltpu.VMEM((layers, toks, depth), bf16), dma((layers // per,)), dma(())],
            compiler_params=pltpu.CompilerParams(vmem_limit_bytes=20 * 1024 * 1024),
            name='norm',
        )(grads, w_t, d_router)
        d_router = d_router.reshape(layers, num_exp, depth).transpose(0, 2, 1)
        return loss[0, 0], d_router, d_norm

    tok_spec = P(None, 'dp', None)
    return jax.shard_map(local_step, mesh=mesh,
                         in_specs=(tok_spec, tok_spec, P(None, 'dp', None, None), tok_spec, P()),
                         out_specs=(P(), P(), tok_spec), check_vma=False)
```

time: 277 us -> 70 us (0.25)
  waiting for transfers between devices: 135 us -> 0 us
  matrix products: 74.2 us -> 0 us
  Pallas kernels: 0 us -> 68.1 us
  blocking collectives: 42.1 us -> 0 us
  between operations: 16.5 us -> 1.82 us
  local copies, waits for them, and re-layouts: 6.52 us -> 0.01 us
    psum x1 -> x0, waiting for transfers between devices: 135 us -> none  [local_step(): d_router = lax.psum(part_grad, 'dp')]
    dot_general x4 -> x0, matrix products: 74.2 us -> none  [the longest x1 56.1 us: router_forward(): jnp.einsum('ltkd,ltd->ltk', expert_out, d_out, preferred_element_type=jnp...]
    pallas_call x0 -> x2, Pallas kernels: none -> 68.1 us  [the longest x1 63 us: local_step(): pl.pallas_call(functools.partial(ring_kernel, dims), out_shape=(pltpu.VME...]
    psum x1 -> x0, blocking collectives: 42.1 us -> none  [local_step(): total_loss = lax.psum(main_part, 'dp') + aux_total]
    unnamed x5 -> x2, local copies, waits for them, and re-layouts: 6.19 us -> 0.01 us
  transfers between devices with their start and end apart: 1 -> 0, of which waited for: 1 -> 0; matrix products, arithmetic and copies ran while one was open for 2% -> 0% of each run, Pallas kernels for 0% -> 0%
where the time goes in v2:
time: 70 us; the launch traced here: 69.9 us
  Pallas kernels  68.1 us (97%)
  between operations  1.82 us (3%)
    pallas_call x1, Pallas kernels, local_step(): pl.pallas_call(functools.partial(ring_kernel, dims), out_shape=(pltpu.VME...  63 us
    pallas_call x1, Pallas kernels, local_step(): pl.pallas_call(functools.partial(norm_kernel, per), out_shape=(jax.ShapeD...  5.09 us

profile of v2, /device:TPU:0, one launch (start us, length us, event | category | flops | bytes accessed | tf_op | source)
XLA Modules:
  0.0 69.9 jit_solution(15326414708282886613)
XLA Ops:
  0.6 0.0 copy-start
  0.6 63.0 %ring.1 = (f32[16,2,8,4096]{3,2,1,0:T(8,128)S(1)}, bf16[16,16,64]{2,1,0:T(8,128)(2,1)S(1)}, f32[1,128]{1,0:T(1,128)S(1)}) custom-call(s32[16,2,64]{2,1,0:T(2,128)} %bitcast.22, bf16[16,64,4096]{2,1,0:T(8,128)(2,1)} %u_hbm.1, bf16[16,16,4096]{2,1,0:T(8,128)(2,1)} %bitcast.17, bf16[16,4096,128]{2,1,0:T(8,128)(2,1)} %bitcast.20, bf16[16,2048,128]{2,1,0:T(8,128)(2,1)} %bitcast.21), custom_call_target="tpu_custom_call" | custom-call | tf_op jit(solution)/shard_map/ring/pallas_call | solution.py:356
  63.6 0.0 copy-done
  63.6 5.1 %norm.1 = (bf16[16,64,4096]{2,1,0:T(8,128)(2,1)}, f32[16,2,8,4096]{3,2,1,0:T(8,128)}) custom-call(bf16[16,16,64]{2,1,0:T(8,128)(2,1)S(1)} %get-tuple-element.9.g_ref, bf16[16,16,4096]{2,1,0:T(8,128)(2,1)S(1)} %bitcast.18, f32[16,2,8,4096]{3,2,1,0:T(8,128)S(1)} %get-tuple-element.10.dr_ref), custom_call_target="tpu_custom_call" | custom-call | tf_op jit(solution)/shard_map/norm/pallas_call | solution.py:369
Async XLA Ops:
  0.6 63.0 %copy-start = (bf16[16,4096,16]{1,2,0:T(8,128)(2,1)S(1)}, bf16[16,4096,16]{1,2,0:T(8,128)(2,1)}, u32[]{:S(2)}) copy-start(bf16[16,4096,16]{1,2,0:T(8,128)(2,1)} %param.9) | copy-start | bytes 6291460

commit v3 on v2

--- a/solution.py
+++ b/solution.py
@@ -14,10 +14,11 @@
 GREET = 2
 BITS = {'c': 1, 'x': 2, 'y': 4, 'p': 8, 'q': 16}
 ORDERS = ('xpyq', 'ypxq') * 8
-T_START, T_FWD, T_BWD, T_COUNTS = 1.5, 0.85, 0.5, 12.5
+T_START, T_GREETED, T_COUNTS = 1.5, 7.5, 13.0
+T_FWD, T_BWD, T_NORM = 0.72, 0.6, 0.35
 T_STAGE = (0.1, 0.08, 0.06, 0.05, 0.05, 0.04, 0.04, 0.04, 0.04, 0.03)
-DELAY = {'c': 1.5, 'x': 3.0, 'y': 3.0, 'p': 3.0, 'q': 3.5}
-AHEAD = 1.5
+DELAY = {'c': 1.53, 'x': 2.98, 'y': 2.98, 'p': 2.98, 'q': 3.4}
+AHEAD = 3
 PRIO = 3
 
 
@@ -28,7 +29,7 @@
     sizes = sizes + sizes[::-1]
     link = dict.fromkeys('cxypm', 0.0)
     arrive, plan = {}, []
-    now, done_f, done_b = T_START, 0, 0
+    now, done_f, done_b, done_n = T_START, 0, 0, 0
 
     def send(i, l):
         axis, cost = paths[l][i], sizes[i]
@@ -72,8 +73,14 @@
             now += T_FWD
             plan.append(('forward', done_f))
             done_f += 1
+            if done_f == GREET:
+                now = max(now, T_GREETED)
         elif now < T_COUNTS:
             now = T_COUNTS
+        elif done_n < done_b and (done_b == layers or min(arrive.values(), default=now + 9) > now + T_NORM):
+            now += T_NORM
+            plan.append(('norm', done_n))
+            done_n += 1
         elif arrive:
             now = min(arrive.values())
             if done_b < layers:
@@ -83,8 +90,8 @@
             return plan
 
 
-def ring_kernel(dims, idx_hbm, u_hbm, w_hbm, e_hbm, d_hbm, out_ref, g_ref, loss_ref,
-                idx_ref, u_all, w_all, e_buf, d_buf, wide, p_all, a_all, part, r0, r1, r2, r3, r4,
+def ring_kernel(dims, idx_hbm, u_hbm, w_hbm, e_hbm, d_hbm, out_ref, dn_ref, loss_ref,
+                idx_ref, u_all, w_all, e_buf, d_buf, wide, p_all, a_all, g_ref, part, r0, r1, r2, r3, r4,
                 cnt_src, cnt_buf, loss_src, loss_buf, loss_acc, pull_row,
                 i_sem, u_sem, w_sem, e_sem, d_sem, *sems):
     layers, toks, num_exp, depth, top_k, group = dims
@@ -243,6 +250,10 @@
             loss_src[...] = mine
             loss_buf[me] = mine
             everyone(loss_src, loss_buf, ls, lv)
+
+    def norm(l):
+        dn_ref[l] = lax.dot_general(g_ref[l], w_all[l], (((0,), (0,)), ((), ())),
+                                    preferred_element_type=jnp.float32).astype(jnp.bfloat16)
 
     def arrived(i, l):
         order = ORDERS[l]
@@ -291,6 +302,8 @@
             get_counts()
         elif kind == 'backward':
             backward(l)
+        elif kind == 'norm':
+            norm(l)
         else:
             arrived(kind, l)
         at += 1
@@ -303,21 +316,18 @@
     loss_ref[...] = jnp.sum(loss_buf[...], axis=0)
 
 
-def norm_kernel(per, g_ref, w_ref, dr_ref, dn_hbm, dr_hbm, buf, dn_sem, dr_sem):
-    layers = g_ref.shape[0]
-    move = pltpu.make_async_copy(dr_ref, dr_hbm, dr_sem)
-    move.start()
-
-    def put(b):
-        return pltpu.make_async_copy(buf.at[pl.ds(b * per, per)], dn_hbm.at[pl.ds(b * per, per)], dn_sem.at[b])
-    for b in range(layers // per):
-        for l in range(b * per, b * per + per):
-            buf[l] = lax.dot_general(g_ref[l], w_ref[l], (((0,), (0,)), ((), ())),
-                                     preferred_element_type=jnp.float32).astype(jnp.bfloat16)
-        put(b).start()
-    for b in range(layers // per):
-        put(b).wait()
-    move.wait()
+def put_kernel(parts, dn_ref, dr_ref, dn_hbm, dr_hbm, sem):
+    layers = dn_ref.shape[0]
+    per = layers // parts
+    copies = []
+    for b in range(parts):
+        at = pl.ds(b * per, per)
+        copies.append(pltpu.make_async_copy(dn_ref.at[at], dn_hbm.at[at], sem.at[2 * b]))
+        copies.append(pltpu.make_async_copy(dr_ref.at[at], dr_hbm.at[at], sem.at[2 * b + 1]))
+    for copy in copies:
+        copy.start()
+    for copy in copies:
+        copy.wait()
 
 
 def solution(mesh):
@@ -345,6 +355,7 @@
             pltpu.VMEM((SLOTS, toks * tiles * top_k, 128), bf16), pltpu.VMEM((SLOTS, toks * tiles, 128), bf16),
             pltpu.VMEM((toks * F_STRIDE, 128), f32),
             pltpu.VMEM((layers, num_exp, toks), f32), pltpu.VMEM((layers, num_exp, toks), f32),
+            pltpu.VMEM((layers, num_exp, toks), bf16),
             pltpu.VMEM((layers, 2, 8, depth), f32), pltpu.VMEM((layers, 8, depth), f32),
             pltpu.VMEM((layers, 8, depth // 2), f32), pltpu.VMEM((layers, 8, depth // 4), f32),
             pltpu.VMEM((layers, 8, depth // 8), f32), pltpu.VMEM((layers, 8, depth // 16), f32),
@@ -353,29 +364,29 @@
             pltpu.VMEM((1, num_exp * layers), f32),
             dma(()), dma((SLOTS,)), dma((SLOTS,)), dma((SLOTS,)), dma((SLOTS,)),
         ] + [dma(())] * 10 + [dma((layers,))] * 10 + [dma(())] * 4
-        d_router, grads, loss = pl.pallas_call(
+        d_router, d_norm, loss = pl.pallas_call(
             functools.partial(ring_kernel, dims),
-            out_shape=(pltpu.VMEM((layers, 2, 8, depth), f32), pltpu.VMEM((layers, num_exp, toks), bf16),
+            out_shape=(pltpu.VMEM((layers, 2, 8, depth), f32), pltpu.VMEM((layers, toks, depth), bf16),
                        pltpu.VMEM((1, 128), f32)),
             in_specs=[hbm, hbm, hbm, hbm, hbm],
             out_specs=(vmem, vmem, vmem),
             scratch_shapes=scratch,
             compiler_params=pltpu.CompilerParams(collective_id=0, has_side_effects=True,
-                                                 vmem_limit_bytes=48 * 1024 * 1024),
+                                                 vmem_limit_bytes=40 * 1024 * 1024),
             name='ring',
         )(pltpu.with_memory_space_constraint(idx_t, pltpu.HBM), u_norm, pltpu.with_memory_space_constraint(w_t, pltpu.HBM), e_rows, d_rows)
 
-        per = 2
+        parts = 4
         d_norm, d_router = pl.pallas_call(
-            functools.partial(norm_kernel, per),
+            functools.partial(put_kernel, parts),
             out_shape=(jax.ShapeDtypeStruct((layers, toks, depth), bf16),
                        jax.ShapeDtypeStruct((layers, 2, 8, depth), f32)),
-            in_specs=[vmem, vmem, vmem],
+            in_specs=[vmem, vmem],
             out_specs=(hbm, hbm),
-            scratch_shapes=[pltpu.VMEM((layers, toks, depth), bf16), dma((layers // per,)), dma(())],
-            compiler_params=pltpu.CompilerParams(vmem_limit_bytes=20 * 1024 * 1024),
-            name='norm',
-        )(grads, w_t, d_router)
+            scratch_shapes=[dma((2 * parts,))],
+            compiler_params=pltpu.CompilerParams(vmem_limit_bytes=1024 * 1024),
+            name='put',
+        )(d_norm, d_router)
         d_router = d_router.reshape(layers, num_exp, depth).transpose(0, 2, 1)
         return loss[0, 0], d_router, d_norm
 

time: 70 us -> 68.6 us (0.980)
  Pallas kernels: 68.1 us -> 66.7 us
    pallas_call x1, Pallas kernels: 63 us -> 62 us  [local_step(): pl.pallas_call(functools.partial(ring_kernel, dims), out_shape=(pltpu.VME...]
where the time goes in v3:
time: 68.6 us; the launch traced here: 68.5 us
  Pallas kernels  66.7 us (97%)
  between operations  1.81 us (3%)
    pallas_call x1, Pallas kernels, local_step(): pl.pallas_call(functools.partial(ring_kernel, dims), out_shape=(pltpu.VME...  62 us
    pallas_call x1, Pallas kernels, local_step(): pl.pallas_call(functools.partial(put_kernel, parts), out_shape=(jax.Shape...  4.66 us

profile of v3, /device:TPU:0, one launch (start us, length us, event | category | flops | bytes accessed | tf_op | source)
XLA Modules:
  0.0 68.5 jit_solution(7853654488704109632)
XLA Ops:
  0.6 62.0 %ring.1 = (f32[16,2,8,4096]{3,2,1,0:T(8,128)S(1)}, bf16[16,64,4096]{2,1,0:T(8,128)(2,1)S(1)}, f32[1,128]{1,0:T(1,128)S(1)}) custom-call(s32[16,2,64]{2,1,0:T(2,128)} %bitcast.21, bf16[16,64,4096]{2,1,0:T(8,128)(2,1)} %u_hbm.1, bf16[16,16,4096]{2,1,0:T(8,128)(2,1)} %bitcast.20, bf16[16,4096,128]{2,1,0:T(8,128)(2,1)} %bitcast.18, bf16[16,2048,128]{2,1,0:T(8,128)(2,1)} %bitcast.19), custom_call_target="tpu_custom_call" | custom-call | tf_op jit(solution)/shard_map/ring/pallas_call | solution.py:367
  62.7 4.7 %put.1 = (bf16[16,64,4096]{2,1,0:T(8,128)(2,1)}, f32[16,2,8,4096]{3,2,1,0:T(8,128)}) custom-call(bf16[16,64,4096]{2,1,0:T(8,128)(2,1)S(1)} %get-tuple-element.9.dn_ref, f32[16,2,8,4096]{3,2,1,0:T(8,128)S(1)} %get-tuple-element.10.dr_ref), custom_call_target="tpu_custom_call" | custom-call | tf_op jit(solution)/shard_map/put/pallas_call | solution.py:380

commit v4 on v3

--- a/solution.py
+++ b/solution.py
@@ -13,12 +13,12 @@
 SLOTS = 6
 GREET = 2
 BITS = {'c': 1, 'x': 2, 'y': 4, 'p': 8, 'q': 16}
-ORDERS = ('xpyq', 'ypxq') * 8
+ORDERS = ('xypq', 'yxpq', 'pqxy', 'xypq', 'yxpq') * 3 + ('xypq',)
 T_START, T_GREETED, T_COUNTS = 1.5, 7.5, 13.0
 T_FWD, T_BWD, T_NORM = 0.72, 0.6, 0.35
 T_STAGE = (0.1, 0.08, 0.06, 0.05, 0.05, 0.04, 0.04, 0.04, 0.04, 0.03)
 DELAY = {'c': 1.53, 'x': 2.98, 'y': 2.98, 'p': 2.98, 'q': 3.4}
-AHEAD = 3
+AHEAD = 2.5
 PRIO = 3
 
 
@@ -28,20 +28,25 @@
     sizes = [2.8 / 2 ** i for i in range(5)]
     sizes = sizes + sizes[::-1]
     link = dict.fromkeys('cxypm', 0.0)
-    arrive, plan = {}, []
+    arrive, early, plan = {}, {}, []
     now, done_f, done_b, done_n = T_START, 0, 0, 0
 
-    def send(i, l):
-        axis, cost = paths[l][i], sizes[i]
-        if axis == 'c':
-            cost = cost * 0.08
+    def occupy(i, l, share):
+        axis = paths[l][i]
+        cost = sizes[i] * share * (0.08 if axis == 'c' else 1.0)
         lane = 'p' if axis == 'q' else axis
         link[lane] = max(now, link[lane]) + cost
         end = link[lane]
         if axis == 'q':
             link['m'] = max(end - cost, link['m']) + 2 * cost
             end = max(end, link['m'])
-        arrive[i, l] = end + DELAY[axis]
+        return end + DELAY[axis]
+
+    def send(i, l):
+        end = occupy(i, l, 1.0 if i < 6 else 0.5)
+        arrive[i, l] = max(end, early.pop((i, l), 0.0))
+        if 5 <= i < 9:
+            early[i + 1, l] = occupy(i + 1, l, 0.5)
 
     counts = False
     while True:
@@ -215,21 +220,33 @@
     def lanes(start, size):
         return pl.ds(start if isinstance(start, int) else pl.multiple_of(start, piece), size)
 
-    def exchange(i, l):
-        order = ORDERS[l]
-        axis = ('c' + order + order[::-1] + 'c')[i]
-        offs = kept[order]
-        if i == 0:
-            src, dst = part.at[l, 1 - core], r0.at[l]
-        elif i < 5:
-            size = depth >> i
-            src = part.at[l, core, :, lanes(offs[i - 1] + (1 - bit[axis]) * size, size)]
-            dst = landing[i].at[l]
-        else:
-            size = depth >> (9 - i)
-            src = dst = out_ref.at[l, core, :, lanes(offs[9 - i], size)]
+    def remote(i, l, src, dst):
+        axis = ('c' + ORDERS[l] + ORDERS[l][::-1] + 'c')[i]
         return pltpu.make_async_remote_copy(src_ref=src, dst_ref=dst, send_sem=send_sems[i], recv_sem=recv_sems[i].at[l],
                                             device_id=(peer[axis],), device_id_type=MESH)
+
+    def scatter(i, l):
+        offs = kept[ORDERS[l]]
+        if i == 0:
+            return remote(i, l, part.at[l, 1 - core], r0.at[l])
+        size = depth >> i
+        src = part.at[l, core, :, lanes(offs[i - 1] + (1 - bit[ORDERS[l][i - 1]]) * size, size)]
+        return remote(i, l, src, landing[i].at[l])
+
+    def gather(i, l):
+        order = ORDERS[l]
+        offs = kept[order]
+        level = 9 - i
+        size = depth >> level
+        if i == 5:
+            parts = [(i, offs[level], size)]
+        else:
+            parts = [(i, offs[level] + (1 - bit[order[level]]) * (size // 2), size // 2)]
+        if i < 9:
+            parts.append((i + 1, offs[level], size))
+        for step, start, width in parts:
+            ref = out_ref.at[l, core, :, lanes(start, width)]
+            remote(step, l, ref, ref).start()
 
     def backward(l):
         at = lax.broadcasted_iota(jnp.int32, (num_exp, num_exp * layers), 1)
@@ -243,7 +260,7 @@
         dw = jnp.dot(grad, u_all[l], preferred_element_type=jnp.float32)
         part[l, 0] = dw[:8]
         part[l, 1] = dw[8:]
-        exchange(0, l).start()
+        scatter(0, l).start()
         if l == layers - 1:
             total = loss_acc[0:1, :] + loss_acc[1:2, :] * (1.0 / tok_all)
             mine = jnp.broadcast_to(jnp.sum(total, axis=1, keepdims=True), (1, 128))
@@ -259,7 +276,7 @@
         order = ORDERS[l]
         offs = kept[order]
         if i < 5:
-            exchange(i, l).wait_recv()
+            scatter(i, l).wait_recv()
             got = landing[i]
             if i < 4:
                 size = depth >> (i + 1)
@@ -268,15 +285,15 @@
                     here = lanes(offs[i] + side * size, size)
                     part[l, core, :, here] += got[l, :, lanes(side * size, size)]
                     if side is not mine:
-                        exchange(i + 1, l).start()
+                        scatter(i + 1, l).start()
             else:
                 here = lanes(offs[4], piece)
                 out_ref[l, core, :, here] = part[l, core, :, here] + got[l]
-                exchange(5, l).start()
+                gather(5, l)
         else:
-            exchange(i, l).wait_recv()
+            drain(landing[9 - i].at[l], recv_sems[i].at[l])
             if i < 9:
-                exchange(i + 1, l).start()
+                gather(i + 1, l)
 
     plan = plan_order(ORDERS)
     n_fwd = 0

time: 68.6 us -> 67 us (0.977)
  Pallas kernels: 66.7 us -> 65 us
    pallas_call x1, Pallas kernels: 62 us -> 60.4 us  [local_step(): pl.pallas_call(functools.partial(ring_kernel, dims), out_shape=(pltpu.VME...]
where the time goes in v4:
time: 67 us; the launch traced here: 66.8 us
  Pallas kernels  65 us (97%)
  between operations  1.81 us (3%)
    pallas_call x1, Pallas kernels, local_step(): pl.pallas_call(functools.partial(ring_kernel, dims), out_shape=(pltpu.VME...  60.4 us
    pallas_call x1, Pallas kernels, local_step(): pl.pallas_call(functools.partial(put_kernel, parts), out_shape=(jax.Shape...  4.66 us

profile of v4, /device:TPU:0, one launch (start us, length us, event | category | flops | bytes accessed | tf_op | source)
XLA Modules:
  0.0 66.8 jit_solution(9129100432756058658)
XLA Ops:
  0.6 60.4 %ring.1 = (f32[16,2,8,4096]{3,2,1,0:T(8,128)S(1)}, bf16[16,64,4096]{2,1,0:T(8,128)(2,1)S(1)}, f32[1,128]{1,0:T(1,128)S(1)}) custom-call(s32[16,2,64]{2,1,0:T(2,128)} %bitcast.21, bf16[16,64,4096]{2,1,0:T(8,128)(2,1)} %u_hbm.1, bf16[16,16,4096]{2,1,0:T(8,128)(2,1)} %bitcast.20, bf16[16,4096,128]{2,1,0:T(8,128)(2,1)} %bitcast.18, bf16[16,2048,128]{2,1,0:T(8,128)(2,1)} %bitcast.19), custom_call_target="tpu_custom_call" | custom-call | tf_op jit(solution)/shard_map/ring/pallas_call | solution.py:384
  61.0 4.7 %put.1 = (bf16[16,64,4096]{2,1,0:T(8,128)(2,1)}, f32[16,2,8,4096]{3,2,1,0:T(8,128)}) custom-call(bf16[16,64,4096]{2,1,0:T(8,128)(2,1)S(1)} %get-tuple-element.9.dn_ref, f32[16,2,8,4096]{3,2,1,0:T(8,128)S(1)} %get-tuple-element.10.dr_ref), custom_call_target="tpu_custom_call" | custom-call | tf_op jit(solution)/shard_map/put/pallas_call | solution.py:397
